TPU v7x, 32 devices: a whole 2x2x4 slice. The times are simulated.
32 devices in a mesh: dom: 4 (over z), ens: 8 (over y, x, core).
Axes of the slice: x: 2, y: 2, z: 4, core: 2. Of those that a mesh axis runs over, the one named last changes fastest.
Arguments:
- ensemble: bfloat16 [128, 1024, 32, 73], P('ens', None, 'dom')
- w_in: bfloat16 [146, 256], replicated
- w_out: bfloat16 [256, 73], replicated
- obs_op: bfloat16 [73, 16], replicated
- obs_val: float32 [1024, 32, 16], P(None, 'dom')
- obs_wt: float32 [1024, 32, 16], P(None, 'dom')
Outputs:
- output: bfloat16 [128, 1024, 32, 73], P('ens', None, 'dom')
All inputs are finite; a program needn't handle non-finite values.
Results may differ from a plain program's by a relative error of at most 0.001.
Values are sent between devices in bfloat16 or wider.
A program may use at most 1 GiB of HBM per device.

v0:
```python
import math
import jax
import jax.numpy as jnp
from jax import lax
from jax.sharding import PartitionSpec as P, NamedSharding

PATCH_SIDE = 8
LOC_RADIUS = 4
NS_STEPS = 20
PRECISE = lax.Precision.HIGHEST


def from_neighbour(send_block, n_dom, offset):
    return lax.ppermute(send_block, 'dom', perm=[(src_idx, (src_idx + offset) % n_dom) for src_idx in range(n_dom)])


def laplacian(ensemble, west_col, east_col):
    center = ensemble.astype(jnp.float32)
    north_nb = jnp.concatenate([center[:, :1], center[:, :-1]], axis=1)
    south_nb = jnp.concatenate([center[:, 1:], center[:, -1:]], axis=1)
    widened = jnp.concatenate([west_col, ensemble, east_col], axis=2).astype(jnp.float32)
    lap_f32 = north_nb + south_nb + widened[:, :, :-2] + widened[:, :, 2:] - 4.0 * center
    return lap_f32.astype(jnp.bfloat16)


def mlp_rows(rows_x, rows_lap, w_in, w_out):
    n_chan = rows_x.shape[-1]
    hidden = jnp.einsum('myxc,cf->myxf', rows_x, w_in[:n_chan], preferred_element_type=jnp.float32)
    hidden = hidden + jnp.einsum('myxc,cf->myxf', rows_lap, w_in[n_chan:], preferred_element_type=jnp.float32)
    act_bf = jax.nn.gelu(hidden).astype(jnp.bfloat16)
    tendency = jnp.einsum('myxf,fc->myxc', act_bf, w_out, preferred_element_type=jnp.float32)
    return (rows_x.astype(jnp.float32) + tendency).astype(jnp.bfloat16)


def value_a15(ensemble, w_in, w_out, n_dom, n_blocks):
    west_col = from_neighbour(ensemble[:, :, -1:], n_dom, 1)
    east_col = from_neighbour(ensemble[:, :, :1], n_dom, -1)
    lap_bf = laplacian(ensemble, west_col, east_col)
    members_dev, n_lat, n_lon, n_chan = ensemble.shape
    blk_shape = (members_dev, n_blocks, n_lat // n_blocks, n_lon, n_chan)
    x_blocks = jnp.moveaxis(ensemble.reshape(blk_shape), 1, 0)
    lap_blocks = jnp.moveaxis(lap_bf.reshape(blk_shape), 1, 0)
    return lax.map(lambda pair_xs: mlp_rows(pair_xs[0], pair_xs[1], w_in, w_out), (x_blocks, lap_blocks))


def obs_windows(packed, west_obs, east_obs):
    n_rec, n_lat, n_lon, n_obs = packed.shape
    blocks = packed.reshape(n_rec, n_lat, n_lon // PATCH_SIDE, PATCH_SIDE, n_obs)
    prev_tail = jnp.concatenate([west_obs[:, :, None], blocks[:, :, :-1, PATCH_SIDE - LOC_RADIUS:]], axis=2)
    next_head = jnp.concatenate([blocks[:, :, 1:, :LOC_RADIUS], east_obs[:, :, None]], axis=2)
    return jnp.concatenate([prev_tail, blocks, next_head], axis=3)


def transform_matrix(yb_win, yo_win, wt_win):
    n_mem = yb_win.shape[0]
    y_mean = jnp.mean(yb_win, axis=0)
    y_anom = yb_win - y_mean
    weighted = y_anom * wt_win
    gram_mat = jnp.einsum('ebypwo,kbypwo->bpek', weighted, y_anom, precision=PRECISE)
    eye_mem = jnp.eye(n_mem, dtype=jnp.float32)
    a_matrix = gram_mat + (n_mem - 1.0) * eye_mem
    trace_a = jnp.trace(a_matrix, axis1=2, axis2=3)[:, :, None, None]

    def ns_step(step_idx, ns_carry):
        y_mat, z_mat = ns_carry
        t_mat = 0.5 * (3.0 * eye_mem - jnp.matmul(z_mat, y_mat, precision=PRECISE))
        return jnp.matmul(y_mat, t_mat, precision=PRECISE), jnp.matmul(t_mat, z_mat, precision=PRECISE)

    init_pair = (a_matrix / trace_a, jnp.broadcast_to(eye_mem, a_matrix.shape))
    ns_out = lax.fori_loop(0, NS_STEPS, ns_step, init_pair)
    s_root = ns_out[1] / jnp.sqrt(trace_a)
    p_ana = jnp.matmul(s_root, s_root, precision=PRECISE)
    cm_innov = jnp.einsum('ebypwo,bypwo->bpe', weighted, yo_win - y_mean, precision=PRECISE)
    w_mean = jnp.einsum('bpek,bpk->bpe', p_ana, cm_innov, precision=PRECISE)
    return math.sqrt(n_mem - 1.0) * s_root + w_mean[..., None]


def analysis(xf_pm, obs_op, obs_rows, wt_rows, n_dom):
    n_mem, n_lat, n_lon, n_chan = xf_pm.shape
    n_obs = obs_op.shape[1]
    n_band = n_lat // PATCH_SIDE
    n_pcol = n_lon // PATCH_SIDE
    win_cols = PATCH_SIDE + 2 * LOC_RADIUS
    ens_obs = jnp.einsum('eyxc,co->eyxo', xf_pm, obs_op, preferred_element_type=jnp.float32)
    packed = jnp.concatenate([ens_obs, obs_rows[None], wt_rows[None]], axis=0)
    west_obs = from_neighbour(packed[:, :, n_lon - LOC_RADIUS:], n_dom, 1)
    east_obs = from_neighbour(packed[:, :, :LOC_RADIUS], n_dom, -1)
    windows = obs_windows(packed, west_obs, east_obs).reshape(n_mem + 2, n_band, PATCH_SIDE, n_pcol, win_cols, n_obs)
    t_full = transform_matrix(windows[:n_mem], windows[n_mem], windows[n_mem + 1])
    xf_f32 = xf_pm.astype(jnp.float32).reshape(n_mem, n_band, PATCH_SIDE, n_pcol, PATCH_SIDE, n_chan)
    x_mean = jnp.mean(xf_f32, axis=0)
    updated = x_mean + jnp.einsum('kbypxc,bpke->ebypxc', xf_f32 - x_mean, t_full, precision=PRECISE)
    return updated.astype(jnp.bfloat16).reshape(n_mem, n_lat, n_lon, n_chan)


def solution(mesh):
    n_dom = mesh.shape['dom']
    n_ens = mesh.shape['ens']

    def local_cycle(ensemble, w_in, w_out, obs_op, obs_val, obs_wt):
        members_dev, n_lat, n_lon, n_chan = ensemble.shape
        lat_dev = n_lat // n_ens
        fcst_blocks = value_a15(ensemble, w_in, w_out, n_dom, n_ens)
        moved_pm = lax.all_to_all(fcst_blocks, 'ens', 0, 0, tiled=True)
        xf_pm = moved_pm.reshape(n_ens * members_dev, lat_dev, n_lon, n_chan)
        row_start = lax.axis_index('ens') * lat_dev
        obs_rows = lax.dynamic_slice_in_dim(obs_val, row_start, lat_dev, axis=0)
        wt_rows = lax.dynamic_slice_in_dim(obs_wt, row_start, lat_dev, axis=0)
        analysed = analysis(xf_pm, obs_op, obs_rows, wt_rows, n_dom)
        back_mm = lax.all_to_all(analysed.reshape(n_ens, members_dev, lat_dev, n_lon, n_chan), 'ens', 0, 0, tiled=True)
        return jnp.moveaxis(back_mm, 0, 1).reshape(members_dev, n_lat, n_lon, n_chan)

    state_spec = P('ens', None, 'dom', None)
    obs_spec = P(None, 'dom', None)
    return jax.shard_map(local_cycle, mesh=mesh, in_specs=(state_spec, P(), P(), P(), obs_spec, obs_spec), out_specs=state_spec, check_vma=False)
```

profile of v0, /device:TPU:0, one launch (start us, length us, event | category | flops | bytes accessed | tf_op | source)
XLA Modules:
  0.0 1573.6 jit_solution(5919937319442552944)
XLA Ops:
  0.0 18.2 %fusion.83 = (bf16[16,1024,1,73]{1,2,3,0:T(2,128)(2,1)S(1)}, bf16[16,1024,1,73]{1,2,3,0:T(2,128)(2,1)S(1)}) fusion(bf16[16,1024,8,73]{1,2,3,0:T(8,128)(2,1)} %param.10), kind=kLoop, calls=%fused_computation.94 | loop fusion | bytes 9568256 | tf_op jit(solution)/shard_map/slice | solution.py:36
  31.6 24.4 %copy.103 = bf16[8,16,128,8,73]{2,4,3,1,0:T(8,128)(2,1)} copy(bf16[8,16,128,8,73]{2,3,0,4,1:T(8,128)(2,1)} %bitcast.171) | data formatting | bytes 38273024 | tf_op jit(solution)/shard_map/while | solution.py:43
  56.0 37.0 %fusion.81 = (f32[16,1023,8,73]{1,2,3,0:T(8,128)}, f32[16,1023,8,73]{1,2,3,0:T(8,128)}) fusion(bf16[16,1024,8,73]{1,2,3,0:T(8,128)(2,1)} %param.10), kind=kLoop, calls=%fused_computation.92 | loop fusion | bytes 152942592 | tf_op jit(solution)/shard_map/slice | solution.py:20
  93.0 7.5 copy.101
  100.5 27.0 %collective-permute-done.1 = bf16[16,1024,1,73]{1,0,3,2:T(8,128)(2,1)} collective-permute-done((bf16[16,1024,1,73]{1,0,3,2:T(8,128)(2,1)}, bf16[16,1024,1,73]{1,0,3,2:T(8,128)(2,1)}, u32[]{:S(2)}, u32[]{:S(2)}) %collective-permute-start.1) | collective-permute-done | bytes 2392096 | tf_op jit(solution)/shard_map/ppermute | solution.py:14
  127.5 7.5 copy.102
  135.1 33.3 %maximum_convert_fusion = f32[16,1024,10,73]{1,2,3,0:T(8,128)} fusion(bf16[16,1024,1,73]{1,2,3,0:T(2,128)(2,1)} %copy.102, bf16[16,1024,8,73]{1,2,3,0:T(8,128)(2,1)} %param.10, bf16[16,1024,1,73]{1,2,3,0:T(2,128)(2,1)} %copy.101), kind=kLoop, calls=%fused_computation.49 | loop fusion | flops 71761920 | bytes 71761920 | tf_op jit(solution)/shard_map/convert_element_type | solution.py:21
  168.4 73.9 %fusion.85 = bf16[8,16,128,8,73]{2,3,0,4,1:T(8,128)(2,1)} fusion(bf16[16,1024,8,73]{1,2,3,0:T(8,128)(2,1)} %param.10, f32[16,1024,10,73]{1,2,3,0:T(8,128)} %maximum_convert_fusion, f32[16,1,8,73]{1,2,3,0:T(8,128)} %get-tuple-element.139, f32[16,1023,8,73]{1,2,3,0:T(8,128)} %get-tuple-element.137, f32[16,1023,8,73]{1,2,3,0:T(8,128)} %get-tuple-element.138, ...), kind=kLoop, calls=%fused_computation.96 | loop fusion | flops 86114304 | bytes 191365120 | tf_op jit(solution)/shard_map/transpose | solution.py:42
  242.2 24.2 %copy.104 = bf16[8,16,128,8,73]{2,4,3,1,0:T(8,128)(2,1)} copy(bf16[8,16,128,8,73]{2,3,0,4,1:T(8,128)(2,1)} %fusion.85) | data formatting | bytes 38273024 | tf_op jit(solution)/shard_map/while | solution.py:43
  266.4 194.0 %while.23 = (s32[]{:T(128)}, bf16[8,16,128,8,73]{2,3,4,1,0:T(8,128)(2,1)}, bf16[8,16,128,8,73]{2,4,3,1,0:T(8,128)(2,1)}, bf16[146,256]{1,0:T(8,128)(2,1)S(1)}, b...) while((s32[]{:T(128)}, bf16[8,16,128,8,73]{2,3,4,1,0:T(8,128)(2,1)}, ...), condition=%wide.region_1.2_spmd, body=%wide.region_0.1_spmd.sunk | while | flops 1882636288 | bytes 48719948 | solution.py:43
  266.8 10.0 fusion.116
  276.9 12.1 fusion.117
  291.0 10.0 fusion.116
  301.0 12.1 fusion.117
  315.2 10.0 fusion.116
  325.2 12.2 fusion.117
  339.5 10.0 fusion.116
  349.5 12.2 fusion.117
  363.8 10.0 fusion.116
  373.8 12.1 fusion.117
  388.0 10.0 fusion.116
  398.0 12.1 fusion.117
  412.1 10.0 fusion.116
  422.1 12.1 fusion.117
  436.3 10.0 fusion.116
  446.3 12.1 fusion.117
  460.4 5.9 all-to-all-start
  469.2 206.5 %all-to-all-done = bf16[8,16,128,8,73]{2,3,4,1,0:T(8,128)(2,1)} async-done(((bf16[8,16,128,8,73]{2,3,4,1,0:T(8,128)(2,1)}), bf16[8,16,128,8,73]{2,3,4,1,0:T(8,128)(2,1)}, u32[]{:S(2)}, u32[]{:S(2)}) %all-to-all-start) | async-done | bytes 19136544 | tf_op jit(solution)/shard_map/all_to_all | solution.py:104
  675.6 11.6 copy.109
  692.3 6.5 fusion.80
  703.0 5.2 collective-permute-start.2
  712.0 8.1 convert_reduce_fusion
  720.4 45.7 %copy.117 = f32[8,16,128,8,73]{4,3,2,1,0:T(8,128)} copy(bf16[8,16,128,8,73]{2,3,4,1,0:T(8,128)(2,1)} %all-to-all-done) | data formatting | bytes 57409536 | tf_op jit(solution)/shard_map/convert_element_type | solution.py:90
  766.2 45.3 %broadcast_subtract_fusion = f32[128,16,8,8,73]{4,3,2,1,0:T(8,128)} fusion(f32[128,16,8,8,73]{4,3,2,1,0:T(8,128)} %bitcast.38, f32[16,8,8,73]{3,2,1,0:T(8,128)S(1)} %bitcast.177), kind=kLoop, calls=%fused_computation.50 | loop fusion | flops 9568256 | bytes 76845056 | tf_op jit(solution)/shard_map/sub | solution.py:92
  811.5 78.7 %collective-permute-done.3 = f32[130,128,4,16]{1,3,2,0:T(8,128)} collective-permute-done((f32[130,128,4,16]{1,3,2,0:T(8,128)}, f32[130,128,4,16]{1,3,2,0:T(8,128)}, u32[]{:S(2)}, u32[]{:S(2)}) %collective-permute-start.3) | collective-permute-done | bytes 4259872 | tf_op jit(solution)/shard_map/ppermute | solution.py:14
  890.2 6.9 pad_maximum_fusion
  898.1 6.6 slice_reduce_fusion
  906.6 17.9 %copy.110 = f32[128,128,1,16,16]{0,4,3,1,2:T(8,128)} copy(f32[128,128,1,16,16]{1,4,3,0,2:T(8,128)} %get-tuple-element.146) | data formatting | bytes 33554432 | tf_op jit(solution)/shard_map/slice | solution.py:89
  927.3 12.5 broadcast_multiply_fusion
  939.8 5.8 copy-done.3
  945.6 13.9 fusion.64
  959.5 33.4 %select_reduce_fusion = (f32[16]{0:T(128)S(1)}, f32[16,128,128]{2,1,0:T(8,128)S(1)}) fusion(pred[128,128]{1,0:T(8,128)(4,1)S(1)} %copy-done.7, f32[128,128]{1,0:T(8,128)S(1)} %copy-done.6, f32[128,16,8,16,16]{0,4,3,2,1:T(8,128)} %get-tuple-element.136, f32[128,16,8,16,16]{0,4,3,2,1:T(8,128)} %copy-done.3), kind=kOutput, calls=%fused_computation.74 | convolution fusion | flops 6443237376 | bytes 34684992 | tf_op jit(solution)/shard_map/ebypwo,kbypwo->bpek/dot_general | solution.py:59
  993.6 110.1 %while.24 = (s32[]{:T(128)}, f32[16,1,128,128]{2,3,0,1:T(8,128)S(1)}, f32[16,1,128,128]{3,2,0,1:T(8,128)S(1)}, s32[]{:T(128)}) while((s32[]{:T(128)}, f32[16,1,128,128]{2,3,0,1:T(8,128)S(1)}, f32[16,1,128,128]{3,2,0,1:T(8,128)S(1)}, s32[]{:T(128)}) %tuple.58), condition=%wide.region_6.7_spmd.clone, body=%wide.region_5.6_spmd.clone.sunk | while | flops 1208516608 | bytes 13762613 | solution.py:70
  1106.8 156.3 %fusion.46 = bf16[128,16,8,1,8,73]{0,5,4,2,1,3:T(8,128)(2,1)} fusion(f32[16,8,8,73]{3,2,1,0:T(8,128)S(1)} %bitcast.178, f32[128,16,8,8,73]{4,3,2,1,0:T(8,128)} %broadcast_subtract_fusion, f32[16,128]{1,0:T(8,128)S(1)} %bitcast.181, f32[16,1,128,128]{3,2,0,1:T(8,128)S(1)} %get-tuple-element.60, f32[16]{0:T(128)S(1)} %sqrt.8), kind=kOutput, calls=%fused_computation.51 | convolution fusion | flops 14716764160 | bytes 58765376 | tf_op jit(solution)/shard_map/kbypxc,bpke->ebypxc/dot_general | solution.py:92
  1263.1 41.8 %copy.119 = bf16[128,16,8,1,8,73]{5,4,2,1,0,3:T(8,128)(2,1)} copy(bf16[128,16,8,1,8,73]{0,5,4,2,1,3:T(8,128)(2,1)} %fusion.46) | data formatting | bytes 38273024 | tf_op jit(solution)/shard_map/convert_element_type | solution.py:93
  1304.9 46.4 %copy.120 = bf16[8,16,128,8,73]{2,3,4,1,0:T(8,128)(2,1)} copy(bf16[8,16,128,8,73]{4,3,2,1,0:T(8,128)(2,1)} %bitcast.172) | data formatting | bytes 38273024 | tf_op jit(solution)/shard_map/reshape;reshape | solution.py:110
  1351.4 213.6 %all_to_all.10 = bf16[8,16,128,8,73]{2,3,4,1,0:T(8,128)(2,1)S(1)} all-to-all(bf16[8,16,128,8,73]{2,3,4,1,0:T(8,128)(2,1)} %copy.120), channel_id=1, replica_groups=mesh['dom'=4,'ens'=8] {'ens'}, dimensions={0} | all-to-all | bytes 38273024 | tf_op jit(solution)/shard_map/all_to_all | solution.py:110
  1565.0 8.4 copy_bitcast_fusion
  (174 shorter events, 164.2 us)
Async XLA Ops:
  0.0 687.3 %copy-start = (bf16[73,16]{0,1:T(8,128)(2,1)S(1)}, bf16[73,16]{0,1:T(8,128)(2,1)}, u32[]{:S(2)}) copy-start(bf16[73,16]{0,1:T(8,128)(2,1)} %param.13) | copy-start | bytes 7012
  0.0 26.8 %copy-start.2 = (bf16[16,1024,8,73]{1,2,3,0:T(8,128)(2,1)S(1)}, bf16[16,1024,8,73]{1,2,3,0:T(8,128)(2,1)}, u32[]{:S(2)}) copy-start(bf16[16,1024,8,73]{1,2,3,0:T(8,128)(2,1)} %param.10) | copy-start | bytes 57409540
  19.1 73.8 %collective-permute-start = (bf16[16,1024,1,73]{1,0,3,2:T(8,128)(2,1)S(1)}, bf16[16,1024,1,73]{1,0,3,2:T(8,128)(2,1)}, u32[]{:S(2)}, u32[]{:S(2)}) collective-permute-start(bf16[16,1024,1,73]{1,0,3,2:T(8,128)(2,1)S(1)} %copy.138), channel_id=1, source_target_pairs={{0,8},{8,16},{16,24},{24,0},{1,9},{9,17},{17,25},{25,1},{2,10},{10... | collective-permute-start | bytes 7176200 | tf_op jit(solution)/shard_map/ppermute | solution.py:14
  24.7 102.8 %collective-permute-start.1 = (bf16[16,1024,1,73]{1,0,3,2:T(8,128)(2,1)}, bf16[16,1024,1,73]{1,0,3,2:T(8,128)(2,1)}, u32[]{:S(2)}, u32[]{:S(2)}) collective-permute-start(bf16[16,1024,1,73]{1,0,3,2:T(8,128)(2,1)} %copy.139), channel_id=1, source_target_pairs={{0,24},{8,0},{16,8},{24,16},{1,25},{9,1},{17,9},{25,17},{2,26},{10... | collective-permute-start | bytes 7176200 | tf_op jit(solution)/shard_map/ppermute | solution.py:14
  242.2 24.2 %copy-start.4 = (bf16[146,256]{1,0:T(8,128)(2,1)S(1)}, bf16[146,256]{1,0:T(8,128)(2,1)}, u32[]{:S(2)}) copy-start(bf16[146,256]{1,0:T(8,128)(2,1)} %param.11) | copy-start | bytes 224260
  242.2 24.2 %copy-start.8 = (bf16[256,73]{0,1:T(8,128)(2,1)S(1)}, bf16[256,73]{0,1:T(8,128)(2,1)}, u32[]{:S(2)}) copy-start(bf16[256,73]{0,1:T(8,128)(2,1)} %param.12) | copy-start | bytes 112132
  460.4 215.2 %all-to-all-start = ((bf16[8,16,128,8,73]{2,3,4,1,0:T(8,128)(2,1)}), bf16[8,16,128,8,73]{2,3,4,1,0:T(8,128)(2,1)}, u32[]{:S(2)}, u32[]{:S(2)}) async-start(bf16[8,16,128,8,73]{2,3,4,1,0:T(8,128)(2,1)} %get-tuple-element.59), calls=%async_computation | async-start | bytes 38273024 | tf_op jit(solution)/shard_map/all_to_all | solution.py:104
  703.0 108.5 %collective-permute-start.2 = (f32[130,128,4,16]{1,3,2,0:T(8,128)}, f32[130,128,4,16]{1,3,2,0:T(8,128)}, u32[]{:S(2)}, u32[]{:S(2)}) collective-permute-start(f32[130,128,4,16]{1,3,2,0:T(8,128)} %get-tuple-element.147), channel_id=1, source_target_pairs={{0,8},{8,16},{16,24},{24,0},{1,9},{9,17},{17,25},{25,1},{2,10},{10... | collective-permute-start | bytes 12779528 | tf_op jit(solution)/shard_map/ppermute | solution.py:14
  708.2 182.0 %collective-permute-start.3 = (f32[130,128,4,16]{1,3,2,0:T(8,128)}, f32[130,128,4,16]{1,3,2,0:T(8,128)}, u32[]{:S(2)}, u32[]{:S(2)}) collective-permute-start(f32[130,128,4,16]{1,3,2,0:T(8,128)} %get-tuple-element.148), channel_id=1, source_target_pairs={{0,24},{8,0},{16,8},{24,16},{1,25},{9,1},{17,9},{25,17},{2,26},{10... | collective-permute-start | bytes 12779528 | tf_op jit(solution)/shard_map/ppermute | solution.py:14
  939.7 5.8 copy-start.3
  939.7 19.7 %copy-start.6 = (f32[128,128]{1,0:T(8,128)S(1)}, f32[128,128]{1,0:T(8,128)}, u32[]{:S(2)}) copy-start(f32[128,128]{1,0:T(8,128)} %fusion.76) | copy-start | bytes 196612
  939.8 19.7 %copy-start.7 = (pred[128,128]{1,0:T(8,128)(4,1)S(1)}, pred[128,128]{1,0:T(8,128)(4,1)}, u32[]{:S(2)}) copy-start(pred[128,128]{1,0:T(8,128)(4,1)} %iota_compare_fusion.1) | copy-start | bytes 49156
  959.5 34.0 %copy-start.5 = (f32[128,128]{1,0:T(8,128)S(1)}, f32[128,128]{1,0:T(8,128)}, u32[]{:S(2)}) copy-start(f32[128,128]{1,0:T(8,128)} %fusion.75) | copy-start | bytes 196612
  1351.4 222.1 %copy-start.1 = (bf16[73,16]{0,1:T(8,128)(2,1)S(1)}, bf16[73,16]{0,1:T(8,128)(2,1)}, u32[]{:S(2)}) copy-start(bf16[73,16]{0,1:T(8,128)(2,1)} %param.13) | copy-start | bytes 7012
where the time goes:
time: 1580 us; the launch traced here: 1570 us
  matrix products  495 us (31%)
  local copies, waits for them, and re-layouts  333 us (21%)
  waiting for transfers between devices  312 us (20%)
  blocking collectives  214 us (14%)
  other arithmetic  198 us (13%)
  starting transfers between devices  20.1 us (1%)
    all_to_all x1, blocking collectives, local_cycle(): lax.all_to_all(analysed.reshape(n_ens, members_dev, lat_dev, n_lon, n_cha...  214 us
    all_to_all x1, waiting for transfers between devices, local_cycle(): moved_pm = lax.all_to_all(fcst_blocks, 'ens', 0, 0, tiled=True)  206 us
    dot_general x1, matrix products, analysis(): jnp.einsum('kbypxc,bpke->ebypxc', xf_f32 - x_mean, t_full, precision=PREC...  156 us
    ppermute x4, waiting for transfers between devices, from_neighbour(): lax.ppermute(send_block, 'dom', perm=[(src_idx, (src_idx + offset) % n_do...  106 us
    dot_general x8, matrix products, mlp_rows(): jnp.einsum('myxf,fc->myxc', act_bf, w_out, preferred_element_type=jnp.flo...  97 us
    dot_general x8, matrix products, mlp_rows(): jnp.einsum('myxc,cf->myxf', rows_x, w_in[:n_chan], preferred_element_type...  80.2 us
    transpose x1, other arithmetic, value_a15(): lap_blocks = jnp.moveaxis(lap_bf.reshape(blk_shape), 1, 0)  73.9 us
    while x2, local copies, waits for them, and re-layouts, value_a15(): lax.map(lambda pair_xs: mlp_rows(pair_xs[0], pair_xs[1], w_in, w_out), (x...  48.6 us
  transfers between devices with their start and end apart: 5, of which 3 were waited for; matrix products, arithmetic and copies ran while one was open for 11% of the time, Pallas kernels for 0%

commit v1 on v0

v1 whole, which is shorter than its diff:
```python
import functools
import math

import jax
import jax.numpy as jnp
from jax import lax
from jax.experimental import pallas as pl
from jax.experimental.pallas import tpu as pltpu
from jax.sharding import PartitionSpec as P

PATCH = 8
OBS = 16
NS_STEPS = 20
CH = 73
CP = 80
KP = 592
HID = 256
MEM = 128
MLOC = 16
LON = 8
PITCH = 24
YL = 32
LATC = 256
NCHUNK = 4
NB = 4
COLS = ((1, 2, 5, 6), (0, 3, 4, 7))

F32 = jnp.float32
BF16 = jnp.bfloat16
INTERPRET = False


def col_of(group, xi):
    a, b = COLS[0][xi], COLS[1][xi]
    if isinstance(group, int):
        return COLS[group][xi]
    return a + group * (b - a)


def lane_swap(tiles, lane):
    low = lane < 64
    even = (lane // 32) % 2 == 0
    t0, t1, t2, t3 = tiles
    a = jnp.where(low, t0, pltpu.roll(t2, 64, 1))
    b = jnp.where(low, pltpu.roll(t0, 64, 1), t2)
    c = jnp.where(low, t1, pltpu.roll(t3, 64, 1))
    d = jnp.where(low, pltpu.roll(t1, 64, 1), t3)
    u0 = jnp.where(even, a, pltpu.roll(c, 32, 1))
    u1 = jnp.where(even, pltpu.roll(a, 96, 1), c)
    u2 = jnp.where(even, b, pltpu.roll(d, 32, 1))
    u3 = jnp.where(even, pltpu.roll(b, 96, 1), d)
    return u0, u1, u2, u3


def edge_kernel(x_ref, w_ref, e_ref, s_ref):
    s_ref[:, CH * 8:, :] = jnp.zeros((2, CP * 8 - CH * 8, 128), F32)
    for m in range(x_ref.shape[0]):
        for c in range(CH):
            for l in range(2):
                s_ref[l, 8 * c:8 * c + 8, :] = x_ref[m, c, :, 128 * l:128 * l + 128].astype(F32)
        for l in range(2):
            for ref, x in ((w_ref, 0), (e_ref, 7)):
                ref[m, :, 128 * l:128 * l + 128] = s_ref.at[l][pl.ds(x, CP, stride=8), :].astype(BF16)


def edge_columns(xt, q):
    nm = 2
    return pl.pallas_call(
        edge_kernel,
        grid=(MLOC // nm,),
        in_specs=[pl.BlockSpec((nm, CH, LON, LATC), lambda i: (i, 0, 0, q))],
        out_specs=[pl.BlockSpec((nm, CP, LATC), lambda i: (i, 0, 0))] * 2,
        out_shape=[jax.ShapeDtypeStruct((MLOC, CP, LATC), BF16)] * 2,
        scratch_shapes=[pltpu.VMEM((2, CP * 8, 128), F32)],
        cost_estimate=pl.CostEstimate(flops=4_000_000_000, bytes_accessed=6_000_000, transcendentals=0),
        name="edge",
        interpret=INTERPRET,
    )(xt)


def forecast_kernel(groups, first, last, *refs):
    halo = 1 in groups
    if halo:
        xc_ref, xl_ref, xr_ref, wh_ref, eh_ref, w1_ref, w2_ref, o_ref, s_ref, r_ref = refs
    else:
        xc_ref, xl_ref, xr_ref, w1_ref, w2_ref, o_ref, s_ref, r_ref = refs
    m = pl.program_id(0)

    @pl.when(m == 0)
    def _():
        s_ref[:, CH * PITCH:, :] = jnp.zeros((4, (CP - CH) * PITCH, 128), F32)

    for c in range(CH):
        row = c * PITCH + 8
        s_ref[0, row:row + 8, :] = xl_ref[0, c, :, :].astype(F32)
        s_ref[1, row:row + 8, :] = xc_ref[0, c, :, 0:128].astype(F32)
        s_ref[2, row:row + 8, :] = xc_ref[0, c, :, 128:256].astype(F32)
        s_ref[3, row:row + 8, :] = xr_ref[0, c, :, :].astype(F32)
    if halo:
        for l in range(2):
            s_ref.at[1 + l][pl.ds(7, CP, stride=PITCH), :] = wh_ref[0, :, 128 * l:128 * l + 128].astype(F32)
            s_ref.at[1 + l][pl.ds(16, CP, stride=PITCH), :] = eh_ref[0, :, 128 * l:128 * l + 128].astype(F32)

    lane = lax.broadcasted_iota(jnp.int32, (16, 128), 1)
    w1 = w1_ref[...]
    w2 = w2_ref[...]

    def column(gi, xi, x):
        feat_x, feat_l = [], []
        for cb in range(CP // 16):
            def slab(l, dx):
                return s_ref.at[l][pl.ds(8 + x + dx + cb * 16 * PITCH, 16, stride=PITCH), :]
            left, c0, c1, right = slab(0, 0), slab(1, 0), slab(2, 0), slab(3, 0)
            c0_n, c1_n = pltpu.roll(c0, 1, 1), pltpu.roll(c1, 1, 1)
            c0_s, c1_s = pltpu.roll(c0, 127, 1), pltpu.roll(c1, 127, 1)
            north0 = jnp.where(lane == 0, c0 if first else pltpu.roll(left, 1, 1), c0_n)
            north1 = jnp.where(lane == 0, c0_n, c1_n)
            south0 = jnp.where(lane == 127, c1_s, c0_s)
            south1 = jnp.where(lane == 127, c1 if last else pltpu.roll(right, 127, 1), c1_s)
            lap0 = north0 + south0 + slab(1, -1) + slab(1, 1) - 4.0 * c0
            lap1 = north1 + south1 + slab(2, -1) + slab(2, 1) - 4.0 * c1
            feat_x.append(jnp.concatenate([c0.astype(BF16), c1.astype(BF16)], axis=1))
            feat_l.append(jnp.concatenate([lap0.astype(BF16), lap1.astype(BF16)], axis=1))
        feats = jnp.concatenate(feat_x + feat_l, axis=0)
        hid = jnp.dot(w1, feats, preferred_element_type=F32)
        inner = hid * (math.sqrt(2.0 / math.pi) + (0.044715 * math.sqrt(2.0 / math.pi)) * (hid * hid))
        half = 0.5 * hid
        act = (half + half * jnp.tanh(inner)).astype(BF16)
        tend = jnp.dot(w2, act, preferred_element_type=F32)
        for l in range(2):
            center = s_ref.at[1 + l][pl.ds(8 + x, CP, stride=PITCH), :]
            r_ref.at[gi * 4 + xi, l][pl.ds(m, CP, stride=PITCH), :] = center + tend[:, 128 * l:128 * l + 128]

    if len(groups) == 1:
        for xi in range(4):
            column(0, xi, col_of(groups[0], xi))
    else:
        def body(gi, carry):
            for xi in range(4):
                column(gi, xi, col_of(gi, xi))
            return carry
        lax.fori_loop(0, 2, body, 0)

    @pl.when(m == MLOC - 1)
    def _():
        def body(c, carry):
            row = pl.multiple_of(c * PITCH, 8)
            for gi in range(len(groups)):
                for l in range(2):
                    tiles = [r_ref[gi * 4 + xi, l, pl.ds(row, 16), :] for xi in range(4)]
                    for j, tile in enumerate(lane_swap(tiles, lane)):
                        o_ref[4 * l + j, gi, c, :, :] = tile.astype(BF16)
            return carry
        lax.fori_loop(0, CH, body, 0)


def forecast(xt, q, groups, halos, w1t, w2t):
    ng = len(groups)
    first, last = q == 0, q == NCHUNK - 1
    lt, rt = max(2 * q - 1, 0), min(2 * q + 2, 2 * NCHUNK - 1)
    specs = [
        pl.BlockSpec((1, CH, LON, LATC), lambda m: (m, 0, 0, q)),
        pl.BlockSpec((1, CH, LON, 128), lambda m: (m, 0, 0, lt)),
        pl.BlockSpec((1, CH, LON, 128), lambda m: (m, 0, 0, rt)),
    ]
    args = [xt, xt, xt]
    if 1 in groups:
        specs += [pl.BlockSpec((1, CP, LATC), lambda m: (m, 0, 0))] * 2
        args += list(halos)
    specs += [pl.BlockSpec(w1t.shape, lambda m: (0, 0)), pl.BlockSpec(w2t.shape, lambda m: (0, 0))]
    return pl.pallas_call(
        functools.partial(forecast_kernel, groups, first, last),
        grid=(MLOC,),
        in_specs=specs,
        out_specs=pl.BlockSpec((8, ng, CH, 16, 128), lambda m: (0, 0, 0, 0, 0)),
        out_shape=jax.ShapeDtypeStruct((8, ng, CH, 16, 128), BF16),
        scratch_shapes=[
            pltpu.VMEM((4, CP * PITCH, 128), F32),
            pltpu.VMEM((ng * 4, 2, CP * PITCH, 128), F32),
        ],
        cost_estimate=pl.CostEstimate(flops=8_000_000_000 * ng, bytes_accessed=10_000_000, transcendentals=0),
        name="forecast",
        interpret=INTERPRET,
    )(*args, w1t, w2t)


def split3(val):
    p1 = val.astype(BF16)
    rest = val - p1.astype(F32)
    p2 = rest.astype(BF16)
    p3 = (rest - p2.astype(F32)).astype(BF16)
    return p1, p2, p3


def gram_kernel(n_in, *refs):
    x_refs = refs[:n_in]
    hk_ref, yo_ref, wt_ref, xt_ref, gl_ref, gr_ref = refs[n_in:]

    def source(g):
        return (x_refs[g], 0) if n_in == 2 else (x_refs[0], g)

    def turned(g, c):
        ref, gi = source(g)
        cols = jnp.concatenate([ref[src, gi, c, :, :] for src in range(8)], axis=0)
        return cols.astype(F32).T

    for g in range(2):
        def pair(cp, carry, g=g):
            top, low = turned(g, 2 * cp), turned(g, 2 * cp + 1)
            row = pl.multiple_of(cp * 16, 16)
            for t in range(16):
                both = jnp.concatenate([top[8 * t:8 * t + 8], low[8 * t:8 * t + 8]], axis=0)
                xt_ref[g * 16 + t, pl.ds(row, 16), :] = both.astype(BF16)
            return carry
        lax.fori_loop(0, CH // 2, pair, 0)
        top = turned(g, CH - 1)
        for t in range(16):
            both = jnp.concatenate([top[8 * t:8 * t + 8], jnp.zeros((8, 128), F32)], axis=0)
            xt_ref[g * 16 + t, KP - 16:KP, :] = both.astype(BF16)

    hk = hk_ref[...]
    for half, out_ref in ((0, gl_ref), (1, gr_ref)):
        def patch_pair(bp, carry, half=half, out_ref=out_ref):
            gram = [None, None]
            innov = [None, None]
            for g in range(2):
                for x2 in range(2):
                    base = g * 16 + (half * 2 + x2) * 4 + bp * 2
                    rhs = jnp.concatenate([xt_ref[base], xt_ref[base + 1]], axis=1)
                    yb = jnp.dot(hk, rhs, preferred_element_type=F32)
                    for i in range(2):
                        ybt = yb[:, 128 * i:128 * i + 128].T
                        mean = jnp.sum(ybt, axis=0, keepdims=True) * (1.0 / MEM)
                        anom = ybt - mean
                        wrow = wt_ref[pl.ds(base + i, 1), :]
                        yrow = yo_ref[pl.ds(base + i, 1), :]
                        cm = anom * wrow
                        inn = cm * (yrow - mean)
                        c1, c2, c3 = split3(cm)
                        p1, p2, p3 = split3(anom)
                        lhs = jnp.concatenate([c3, c1, c2, c2, c1, c1], axis=1)
                        rh = jnp.concatenate([p1, p3, p2, p1, p2, p1], axis=1)
                        part = lax.dot_general(lhs, rh, (((1,), (1,)), ((), ())), preferred_element_type=F32)
                        gram[i] = part if gram[i] is None else gram[i] + part
                        innov[i] = inn if innov[i] is None else innov[i] + inn
            for i in range(2):
                b = bp * 2 + i
                out_ref[b, 0:128, :] = gram[i]
                row = jnp.sum(innov[i].T, axis=0, keepdims=True)
                out_ref[b, 128:136, :] = jnp.broadcast_to(row, (8, 128))
            return carry
        lax.fori_loop(0, NB // 2, patch_pair, 0)


def gram(arrived, hk, yo, wt):
    vm = pl.BlockSpec(memory_space=pltpu.VMEM)
    n_in = len(arrived)
    return pl.pallas_call(
        functools.partial(gram_kernel, n_in),
        in_specs=[vm] * (n_in + 3),
        out_specs=[vm] * 3,
        out_shape=[
            jax.ShapeDtypeStruct((32, KP, 128), BF16),
            jax.ShapeDtypeStruct((NB, 136, 128), F32),
            jax.ShapeDtypeStruct((NB, 136, 128), F32),
        ],
        cost_estimate=pl.CostEstimate(flops=8_000_000_000, bytes_accessed=10_000_000, transcendentals=0),
        name="gram",
        interpret=INTERPRET,
    )(*arrived, hk, yo, wt)


def lhs_of(parts):
    p1, p2, p3 = parts
    return jnp.concatenate([p1, p2], axis=1), jnp.concatenate([p1, p3], axis=1)


def rhs_of(parts):
    p1, p2, p3 = parts
    top = jnp.concatenate([p1, p2], axis=1)
    return jnp.concatenate([top, top], axis=0), jnp.concatenate([p3, p1], axis=0)


def mm(lhs, rhs):
    main = jnp.dot(lhs[0], rhs[0], preferred_element_type=F32)
    tail = jnp.dot(lhs[1], rhs[1], preferred_element_type=F32)
    return main[:, :128] + (main[:, 128:] + tail)


def update_kernel(gl_ref, gr_ref, gw_ref, ge_ref, xt_ref, o_ref, y_ref, z_ref, t_ref, u_ref):
    rows = lax.broadcasted_iota(jnp.int32, (128, 128), 0)
    cols = lax.broadcasted_iota(jnp.int32, (128, 128), 1)
    eye = jnp.where(rows == cols, 1.0, 0.0).astype(F32)
    traces = []
    innovs = []
    for b in range(NB):
        full = (gw_ref[b] + gl_ref[b]) + (gr_ref[b] + ge_ref[b])
        a_mat = full[0:128] + (MEM - 1.0) * eye
        diag = jnp.sum(a_mat * eye, axis=0, keepdims=True)
        trace = jnp.sum(diag, axis=1, keepdims=True)
        traces.append(trace)
        innovs.append(full[128:129])
        y_ref[b] = a_mat / trace
        z_ref[b] = eye

    def step(i, carry):
        for b in range(NB):
            ys, zs = split3(y_ref[b]), split3(z_ref[b])
            u_mat = 0.5 * (3.0 * eye - mm(lhs_of(zs), rhs_of(ys)))
            us = split3(u_mat)
            y_ref[b] = mm(lhs_of(ys), rhs_of(us))
            z_ref[b] = mm(lhs_of(us), rhs_of(zs))
        return carry

    lax.fori_loop(0, NS_STEPS, step, 0)

    for b in range(NB):
        root = z_ref[b] / jnp.sqrt(traces[b])
        parts = split3(root)
        p_ana = mm(lhs_of(parts), rhs_of(parts))
        wbar = jnp.sum(p_ana * innovs[b], axis=1, keepdims=True)
        t_full = math.sqrt(MEM - 1.0) * root + wbar
        col_sum = jnp.sum(t_full, axis=0, keepdims=True)
        t_full = t_full + (1.0 - col_sum) * (1.0 / MEM)
        t1, t2, t3 = split3(t_full)
        t_ref[b] = jnp.concatenate([
            jnp.concatenate([t1, t3], axis=1),
            jnp.concatenate([t2, jnp.zeros_like(t2)], axis=1)], axis=0)

    for g in range(2):
        def apply(xb, carry, g=g):
            field = xt_ref[g * 16 + xb]
            out = jnp.dot(jnp.concatenate([field, field], axis=1), t_ref[lax.rem(xb, NB)], preferred_element_type=F32)
            u_ref[xb] = out[:, :128] + out[:, 128:]
            return carry
        lax.fori_loop(0, 16, apply, 0)

        def turn(c, carry, g=g):
            row = pl.multiple_of(c * 8, 8)
            tile = jnp.concatenate([u_ref[xb, pl.ds(row, 8), :] for xb in range(16)], axis=0)
            back = tile.T.astype(BF16)
            for d in range(8):
                o_ref[d, g, c, :, :] = back[16 * d:16 * d + 16]
            return carry
        lax.fori_loop(0, CH, turn, 0)


def update(g_left, g_right, g_west, g_east, xt):
    vm = pl.BlockSpec(memory_space=pltpu.VMEM)
    return pl.pallas_call(
        update_kernel,
        in_specs=[vm] * 5,
        out_specs=vm,
        out_shape=jax.ShapeDtypeStruct((8, 2, CH, 16, 128), BF16),
        scratch_shapes=[
            pltpu.VMEM((NB, 128, 128), F32),
            pltpu.VMEM((NB, 128, 128), F32),
            pltpu.VMEM((NB, 256, 256), BF16),
            pltpu.VMEM((16, KP, 128), F32),
        ],
        cost_estimate=pl.CostEstimate(flops=12_000_000_000, bytes_accessed=10_000_000, transcendentals=0),
        name="update",
        interpret=INTERPRET,
    )(g_left, g_right, g_west, g_east, xt)


def place_kernel(x_ref, *refs):
    o_ref, s_ref = refs[-2:]
    lane = lax.broadcasted_iota(jnp.int32, (16, 128), 1)

    def body(c, carry):
        for l in range(2):
            for g in range(2):
                tiles = [x_ref[4 * l + j, g, c, :, :].astype(F32) for j in range(4)]
                for xi, tile in enumerate(lane_swap(tiles, lane)):
                    row = COLS[g][xi] * PITCH
                    s_ref[l, row:row + 16, :] = tile
            for m in range(MLOC):
                o_ref[m, c, :, 128 * l:128 * l + 128] = s_ref.at[l][pl.ds(m, 8, stride=PITCH), :].astype(BF16)
        return carry
    lax.fori_loop(0, CH, body, 0)


def place(arrived, q, state):
    vm = pl.BlockSpec(memory_space=pltpu.VMEM)
    args, specs, alias = [arrived], [vm], {}
    if state is not None:
        args.append(state)
        specs.append(pl.BlockSpec(memory_space=pl.ANY))
        alias = {1: 0}
    return pl.pallas_call(
        place_kernel,
        grid=(1,),
        in_specs=[pl.BlockSpec((8, 2, CH, 16, 128), lambda i: (0, 0, 0, 0, 0))] + specs[1:],
        out_specs=pl.BlockSpec((MLOC, CH, LON, LATC), lambda i: (0, 0, 0, q)),
        out_shape=jax.ShapeDtypeStruct((MLOC, CH, LON, LATC * NCHUNK), BF16),
        scratch_shapes=[pltpu.VMEM((2, 8 * PITCH, 128), F32)],
        input_output_aliases=alias,
        cost_estimate=pl.CostEstimate(flops=4_000_000_000, bytes_accessed=10_000_000, transcendentals=0),
        name="place",
        interpret=INTERPRET,
    )(*args)


def shift(block, n_dom, offset):
    return lax.ppermute(block, 'dom', perm=[(s, (s + offset) % n_dom) for s in range(n_dom)])


def obs_rows(obs, me):
    mine = lax.dynamic_index_in_dim(obs.reshape(NCHUNK, 8, NB, PATCH, LON, OBS), me, axis=1, keepdims=False)
    order = COLS[0] + COLS[1]
    mine = jnp.stack([mine[:, :, :, x, :] for x in order], axis=1)
    return jnp.swapaxes(mine, 3, 4).reshape(NCHUNK, 8 * NB, OBS * PATCH)


def weights(w_in, w_out, obs_op):
    z = jnp.zeros((HID, CP - CH), BF16)
    w1t = jnp.concatenate([w_in[:CH].T, z, w_in[CH:].T, z], axis=1)
    w2t = jnp.concatenate([w_out.T, jnp.zeros((CP - CH, HID), BF16)], axis=0)
    hk = jnp.einsum('co,yz->oycz', obs_op, jnp.eye(PATCH, dtype=BF16)).reshape(OBS * PATCH, CH * PATCH)
    hk = jnp.concatenate([hk, jnp.zeros((OBS * PATCH, KP - CH * PATCH), BF16)], axis=1)
    return w1t, w2t, hk


def solution(mesh):
    n_dom = mesh.shape['dom']

    def exchange(block):
        return lax.all_to_all(block, 'ens', 0, 0, tiled=True)

    def local_cycle(ensemble, w_in, w_out, obs_op, obs_val, obs_wt):
        me = lax.axis_index('ens')
        xt = jnp.transpose(ensemble, (0, 3, 2, 1))
        w1t, w2t, hk = weights(w_in, w_out, obs_op)
        yo, wt = obs_rows(obs_val, me), obs_rows(obs_wt, me)

        arrived = []
        for q in range(NCHUNK):
            to_west, to_east = edge_columns(xt, q)
            halos = (shift(to_east, n_dom, 1), shift(to_west, n_dom, -1))
            if q == 0:
                arrived.append([exchange(forecast(xt, q, (g,), halos, w1t, w2t)) for g in (0, 1)])
            else:
                arrived.append([exchange(forecast(xt, q, (0, 1), halos, w1t, w2t))])

        state = None
        for q in range(NCHUNK):
            turned, g_left, g_right = gram(arrived[q], hk, yo[q], wt[q])
            g_west, g_east = shift(g_right, n_dom, 1), shift(g_left, n_dom, -1)
            back = exchange(update(g_left, g_right, g_west, g_east, turned))
            state = place(back, q, state)
        return jnp.transpose(state, (0, 3, 2, 1))

    state_spec = P('ens', None, 'dom', None)
    obs_spec = P(None, 'dom', None)
    return jax.shard_map(local_cycle, mesh=mesh, in_specs=(state_spec, P(), P(), P(), obs_spec, obs_spec),
                         out_specs=state_spec, check_vma=False)
```

time: 1580 us -> 824 us (0.52)
  Pallas kernels: 0 us -> 606 us
  matrix products: 495 us -> 0 us
  local copies, waits for them, and re-layouts: 333 us -> 26.1 us
  blocking collectives: 214 us -> 0 us
  other arithmetic: 198 us -> 1.05 us
  waiting for transfers between devices: 312 us -> 116 us
  starting transfers between devices: 20.1 us -> 72.7 us
    pallas_call x0 -> x21, Pallas kernels: none -> 606 us  [the longest x5 234 us: forecast(): pl.pallas_call(functools.partial(forecast_kernel, groups, first, last), g...]
    dot_general x82 -> x0, matrix products: 495 us -> none  [the longest x1 156 us: analysis(): jnp.einsum('kbypxc,bpke->ebypxc', xf_f32 - x_mean, t_full, precision=PREC...]
    all_to_all x1 -> x0, blocking collectives: 214 us -> none  [local_cycle(): lax.all_to_all(analysed.reshape(n_ens, members_dev, lat_dev, n_lon, n_cha...]
    all_to_all x1 -> x9, waiting for transfers between devices: 206 us -> 2.12 us  [exchange(): return lax.all_to_all(block, 'ens', 0, 0, tiled=True)]
    convert_element_type x2 -> x0, local copies, waits for them, and re-layouts: 87.6 us -> none  [the longest x1 45.7 us: analysis(): xf_pm.astype(jnp.float32)]
    slice x7 -> x13, local copies, waits for them, and re-layouts: 84.8 us -> 2.76 us  [the longest x10 1.04 us: local_cycle(): turned, g_left, g_right = gram(arrived[q], hk, yo[q], wt[q])]
    transpose x1, other arithmetic: 73.9 us -> 0.23 us  [weights(): jnp.einsum('co,yz->oycz', obs_op, jnp.eye(PATCH, dtype=BF16))]
    while x42 -> x0, local copies, waits for them, and re-layouts: 51.4 us -> none  [the longest x2 48.6 us: value_a15(): lax.map(lambda pair_xs: mlp_rows(pair_xs[0], pair_xs[1], w_in, w_out), (x...]
  transfers between devices with their start and end apart: 5 -> 25, of which waited for: 3 -> 15; matrix products, arithmetic and copies ran while one was open for 11% -> 2% of each run, Pallas kernels for 0% -> 67%
where the time goes in v1:
time: 824 us; the launch traced here: 822 us
  Pallas kernels  606 us (74%)
  waiting for transfers between devices  116 us (14%)
  starting transfers between devices  72.7 us (9%)
  local copies, waits for them, and re-layouts  26.1 us (3%)
    pallas_call x5, Pallas kernels, forecast(): pl.pallas_call(functools.partial(forecast_kernel, groups, first, last), g...  234 us
    pallas_call x4, Pallas kernels, update(): pl.pallas_call(update_kernel, in_specs=[vm] * 5, out_specs=vm, out_shape=...  206 us
    ppermute x16, waiting for transfers between devices, shift(): lax.ppermute(block, 'dom', perm=[(s, (s + offset) % n_dom) for s in range...  114 us
    pallas_call x4, Pallas kernels, place(): pl.pallas_call(place_kernel, grid=(1,), in_specs=[pl.BlockSpec((8, 2, CH,...  71 us
    pallas_call x4, Pallas kernels, gram(): pl.pallas_call(functools.partial(gram_kernel, n_in), in_specs=[vm] * (n_i...  69.5 us
    all_to_all x9, starting transfers between devices, exchange(): return lax.all_to_all(block, 'ens', 0, 0, tiled=True)  42.1 us
    ppermute x16, starting transfers between devices, shift(): lax.ppermute(block, 'dom', perm=[(s, (s + offset) % n_dom) for s in range...  30.6 us
    pallas_call x4, Pallas kernels, edge_columns(): pl.pallas_call(edge_kernel, grid=(MLOC // nm,), in_specs=[pl.BlockSpec((n...  25.9 us
  transfers between devices with their start and end apart: 25, of which 15 were waited for; matrix products, arithmetic and copies ran while one was open for 2% of the time, Pallas kernels for 67%

profile of v1, /device:TPU:0, one launch (start us, length us, event | category | flops | bytes accessed | tf_op | source)
XLA Modules:
  0.0 822.4 jit_solution(18421399008703910149)
XLA Ops:
  3.4 33.3 %forecast.8 = bf16[8,1,73,16,128]{4,3,2,1,0:T(8,128)(2,1)} custom-call(bf16[16,73,8,1024]{3,2,1,0:T(8,128)(2,1)} %bitcast.79, bf16[16,73,8,1024]{3,2,1,0:T(8,128)(2,1)} %bitcast.80, bf16[16,73,8,1024]{3,2,1,0:T(8,128)(2,1)} %bitcast.81, bf16[256,160]{1,0:T(8,128)(2,1)} %pad_maximum_fusion.refs_5_.refs_3_, bf16[80,256]{1,0:T(8,128)(2,1)} %concatenate.10.refs_6_.refs_4_), custom_call_target="tpu_custom_call" | custom-call | flops 8000000000 | bytes 10000000 | tf_op jit(solution)/shard_map/forecast/pallas_call | solution.py:171
  36.6 5.2 all-to-all-start.6
  41.9 6.5 edge.7
  52.1 6.4 edge.6
  58.6 3.8 collective-permute-start.9
  62.4 5.4 collective-permute-done.12.refs_3_
  67.8 13.7 %collective-permute-done.13.refs_4_ = bf16[16,80,256]{2,1,0:T(8,128)(2,1)} collective-permute-done((bf16[16,80,256]{2,1,0:T(8,128)(2,1)}, bf16[16,80,256]{2,1,0:T(8,128)(2,1)}, u32[]{:S(2)}, u32[]{:S(2)}) %collective-permute-start.13) | collective-permute-done | bytes 655392 | tf_op jit(solution)/shard_map/ppermute | solution.py:406
  81.5 33.6 %forecast.9 = bf16[8,1,73,16,128]{4,3,2,1,0:T(8,128)(2,1)} custom-call(bf16[16,73,8,1024]{3,2,1,0:T(8,128)(2,1)} %bitcast.84, bf16[16,73,8,1024]{3,2,1,0:T(8,128)(2,1)} %bitcast.85, bf16[16,73,8,1024]{3,2,1,0:T(8,128)(2,1)} %bitcast.86, bf16[16,80,256]{2,1,0:T(8,128)(2,1)} %collective-permute-done.12.refs_3_, ...), custom_call_target="tpu_custom_call" | custom-call | flops 8000000000 | bytes 10000000 | tf_op jit(solution)/shard_map/forecast/pallas_call | solution.py:171
  115.1 4.4 all-to-all-start.7
  120.4 55.8 %forecast.7 = bf16[8,2,73,16,128]{4,3,2,1,0:T(8,128)(2,1)} custom-call(bf16[16,73,8,1024]{3,2,1,0:T(8,128)(2,1)} %bitcast.87, bf16[16,73,8,1024]{3,2,1,0:T(8,128)(2,1)} %bitcast.88, bf16[16,73,8,1024]{3,2,1,0:T(8,128)(2,1)} %bitcast.89, bf16[16,80,256]{2,1,0:T(8,128)(2,1)} %copy-done.3, bf16[16,80,256]{2,1,0:T(8,128)(2,1)} %collective-permute-done.9.refs_4_, ...), custom_call_target="tpu_custom_call" | custom-call | flops 16000000000 | bytes 10000000 | tf_op jit(solution)/shard_map/forecast/pallas_call | solution.py:171
  176.1 4.7 all-to-all-start.4
  180.8 6.4 edge.5
  188.0 3.0 collective-permute-start.5
  191.0 15.7 %collective-permute-done.4.refs_3_ = bf16[16,80,256]{2,1,0:T(8,128)(2,1)S(1)} collective-permute-done((bf16[16,80,256]{2,1,0:T(8,128)(2,1)}, bf16[16,80,256]{2,1,0:T(8,128)(2,1)S(1)}, u32[]{:S(2)}, u32[]{:S(2)}) %collective-permute-start.4) | collective-permute-done | bytes 655392 | tf_op jit(solution)/shard_map/ppermute | solution.py:406
  206.7 11.8 %collective-permute-done.5.refs_4_ = bf16[16,80,256]{2,1,0:T(8,128)(2,1)S(1)} collective-permute-done((bf16[16,80,256]{2,1,0:T(8,128)(2,1)}, bf16[16,80,256]{2,1,0:T(8,128)(2,1)S(1)}, u32[]{:S(2)}, u32[]{:S(2)}) %collective-permute-start.5) | collective-permute-done | bytes 655392 | tf_op jit(solution)/shard_map/ppermute | solution.py:406
  219.3 55.8 %forecast.6 = bf16[8,2,73,16,128]{4,3,2,1,0:T(8,128)(2,1)} custom-call(bf16[16,73,8,1024]{3,2,1,0:T(8,128)(2,1)} %bitcast.91, bf16[16,73,8,1024]{3,2,1,0:T(8,128)(2,1)} %bitcast.92, bf16[16,73,8,1024]{3,2,1,0:T(8,128)(2,1)} %bitcast.93, bf16[16,80,256]{2,1,0:T(8,128)(2,1)} %copy-done.4, bf16[16,80,256]{2,1,0:T(8,128)(2,1)} %copy-done.5, ...), custom_call_target="tpu_custom_call" | custom-call | flops 16000000000 | bytes 10000000 | tf_op jit(solution)/shard_map/forecast/pallas_call | solution.py:171
  275.1 4.6 all-to-all-start.2
  279.7 6.5 edge.4
  287.1 2.9 collective-permute-start.1
  292.7 2.7 copy.52
  297.4 8.4 %collective-permute-done.refs_3_ = bf16[16,80,256]{2,1,0:T(8,128)(2,1)S(1)} collective-permute-done((bf16[16,80,256]{2,1,0:T(8,128)(2,1)}, bf16[16,80,256]{2,1,0:T(8,128)(2,1)S(1)}, u32[]{:S(2)}, u32[]{:S(2)}) %collective-permute-start) | collective-permute-done | bytes 655392 | tf_op jit(solution)/shard_map/ppermute | solution.py:406
  305.7 12.0 %collective-permute-done.1.refs_4_ = bf16[16,80,256]{2,1,0:T(8,128)(2,1)S(1)} collective-permute-done((bf16[16,80,256]{2,1,0:T(8,128)(2,1)}, bf16[16,80,256]{2,1,0:T(8,128)(2,1)S(1)}, u32[]{:S(2)}, u32[]{:S(2)}) %collective-permute-start.1) | collective-permute-done | bytes 655392 | tf_op jit(solution)/shard_map/ppermute | solution.py:406
  318.6 55.4 %forecast.5 = bf16[8,2,73,16,128]{4,3,2,1,0:T(8,128)(2,1)} custom-call(bf16[16,73,8,1024]{3,2,1,0:T(8,128)(2,1)} %bitcast.95, bf16[16,73,8,1024]{3,2,1,0:T(8,128)(2,1)} %bitcast.96, bf16[16,73,8,1024]{3,2,1,0:T(8,128)(2,1)} %bitcast.97, bf16[16,80,256]{2,1,0:T(8,128)(2,1)} %copy-done.1, bf16[16,80,256]{2,1,0:T(8,128)(2,1)} %copy-done.2, ...), custom_call_target="tpu_custom_call" | custom-call | flops 16000000000 | bytes 10000000 | tf_op jit(solution)/shard_map/forecast/pallas_call | solution.py:171
  374.0 4.8 all-to-all-start
  384.8 17.3 %gram.7 = (bf16[32,592,128]{2,1,0:T(8,128)(2,1)}, f32[4,136,128]{2,1,0:T(8,128)}, f32[4,136,128]{2,1,0:T(8,128)}) custom-call(bf16[8,1,73,16,128]{4,3,2,1,0:T(8,128)(2,1)} %copy-done, bf16[8,1,73,16,128]{4,3,2,1,0:T(8,128)(2,1)} %all-to-all-done.7.refs_1_, bf16[128,592]{1,0:T(8,128)(2,1)} %concatenate.11.refs_1_.refs_2_, f32[32,128]{1,0:T(8,128)} %squeeze.39.refs_3_, ...), custom_call_target="tpu_custom_call" | custom-call | flops 8000000000 | bytes 10000000 | tf_op jit(solution)/shard_map/gram/pallas_call | solution.py:258
  406.0 7.7 collective-permute-done.14.gw_ref
  413.6 4.3 collective-permute-done.15.ge_ref
  418.7 51.5 %update.7 = bf16[8,2,73,16,128]{4,3,2,1,0:T(8,128)(2,1)} custom-call(f32[4,136,128]{2,1,0:T(8,128)} %get-tuple-element.42.gl_ref, f32[4,136,128]{2,1,0:T(8,128)} %get-tuple-element.43.gr_ref, f32[4,136,128]{2,1,0:T(8,128)} %copy-done.9, f32[4,136,128]{2,1,0:T(8,128)} %copy-done.13, bf16[32,592,128]{2,1,0:T(8,128)(2,1)} %get-tuple-element.44.xt_ref), custom_call_target="tpu_custom_call" | custom-call | flops 12000000000 | bytes 10000000 | tf_op jit(solution)/shard_map/update/pallas_call | solution.py:350
  470.1 4.6 all-to-all-start.8
  476.5 17.4 %gram.6 = (bf16[32,592,128]{2,1,0:T(8,128)(2,1)}, f32[4,136,128]{2,1,0:T(8,128)}, f32[4,136,128]{2,1,0:T(8,128)}) custom-call(bf16[8,2,73,16,128]{4,3,2,1,0:T(8,128)(2,1)} %all-to-all-done.4.refs_0_, bf16[128,592]{1,0:T(8,128)(2,1)} %concatenate.11.refs_1_.refs_2_, f32[32,128]{1,0:T(8,128)} %squeeze.37.refs_2_, f32[32,128]{1,0:T(8,128)} %squeeze.38.refs_3_), custom_call_target="tpu_custom_call" | custom-call | flops 8000000000 | bytes 10000000 | tf_op jit(solution)/shard_map/gram/pallas_call | solution.py:258
  497.7 7.6 collective-permute-done.10.gw_ref
  505.4 4.1 collective-permute-done.11.ge_ref
  510.2 51.4 %update.6 = bf16[8,2,73,16,128]{4,3,2,1,0:T(8,128)(2,1)} custom-call(f32[4,136,128]{2,1,0:T(8,128)} %get-tuple-element.37.gl_ref, f32[4,136,128]{2,1,0:T(8,128)} %get-tuple-element.38.gr_ref, f32[4,136,128]{2,1,0:T(8,128)} %copy-done.10, f32[4,136,128]{2,1,0:T(8,128)} %copy-done.14, bf16[32,592,128]{2,1,0:T(8,128)(2,1)} %get-tuple-element.39.xt_ref), custom_call_target="tpu_custom_call" | custom-call | flops 12000000000 | bytes 10000000 | tf_op jit(solution)/shard_map/update/pallas_call | solution.py:350
  561.6 4.6 all-to-all-start.5
  568.0 17.4 %gram.5 = (bf16[32,592,128]{2,1,0:T(8,128)(2,1)}, f32[4,136,128]{2,1,0:T(8,128)}, f32[4,136,128]{2,1,0:T(8,128)}) custom-call(bf16[8,2,73,16,128]{4,3,2,1,0:T(8,128)(2,1)} %all-to-all-done.2.refs_0_, bf16[128,592]{1,0:T(8,128)(2,1)} %concatenate.11.refs_1_.refs_2_, f32[32,128]{1,0:T(8,128)} %squeeze.35.refs_2_, f32[32,128]{1,0:T(8,128)} %squeeze.36.refs_3_), custom_call_target="tpu_custom_call" | custom-call | flops 8000000000 | bytes 10000000 | tf_op jit(solution)/shard_map/gram/pallas_call | solution.py:258
  589.2 7.6 collective-permute-done.6.gw_ref
  596.8 4.1 collective-permute-done.7.ge_ref
  601.6 51.5 %update.5 = bf16[8,2,73,16,128]{4,3,2,1,0:T(8,128)(2,1)} custom-call(f32[4,136,128]{2,1,0:T(8,128)} %get-tuple-element.32.gl_ref, f32[4,136,128]{2,1,0:T(8,128)} %get-tuple-element.33.gr_ref, f32[4,136,128]{2,1,0:T(8,128)} %copy-done.11, f32[4,136,128]{2,1,0:T(8,128)} %copy-done.15, bf16[32,592,128]{2,1,0:T(8,128)(2,1)} %get-tuple-element.34.xt_ref), custom_call_target="tpu_custom_call" | custom-call | flops 12000000000 | bytes 10000000 | tf_op jit(solution)/shard_map/update/pallas_call | solution.py:350
  653.1 4.6 all-to-all-start.3
  659.5 17.4 %gram.4 = (bf16[32,592,128]{2,1,0:T(8,128)(2,1)}, f32[4,136,128]{2,1,0:T(8,128)}, f32[4,136,128]{2,1,0:T(8,128)}) custom-call(bf16[8,2,73,16,128]{4,3,2,1,0:T(8,128)(2,1)} %all-to-all-done.refs_0_, bf16[128,592]{1,0:T(8,128)(2,1)} %concatenate.11.refs_1_.refs_2_, f32[32,128]{1,0:T(8,128)} %squeeze.32.refs_2_, f32[32,128]{1,0:T(8,128)} %squeeze.34.refs_3_), custom_call_target="tpu_custom_call" | custom-call | flops 8000000000 | bytes 10000000 | tf_op jit(solution)/shard_map/gram/pallas_call | solution.py:258
  680.7 7.6 collective-permute-done.2.gw_ref
  688.4 4.1 collective-permute-done.3.ge_ref
  693.2 51.5 %update.4 = bf16[8,2,73,16,128]{4,3,2,1,0:T(8,128)(2,1)} custom-call(f32[4,136,128]{2,1,0:T(8,128)} %get-tuple-element.27.gl_ref, f32[4,136,128]{2,1,0:T(8,128)} %get-tuple-element.28.gr_ref, f32[4,136,128]{2,1,0:T(8,128)} %copy-done.12, f32[4,136,128]{2,1,0:T(8,128)} %copy-done.16, bf16[32,592,128]{2,1,0:T(8,128)(2,1)} %get-tuple-element.29.xt_ref), custom_call_target="tpu_custom_call" | custom-call | flops 12000000000 | bytes 10000000 | tf_op jit(solution)/shard_map/update/pallas_call | solution.py:350
  744.7 4.6 all-to-all-start.1
  749.3 17.7 %place.4.refs_0_ = bf16[16,73,8,1024]{3,2,1,0:T(8,128)(2,1)} custom-call(bf16[8,2,73,16,128]{4,3,2,1,0:T(8,128)(2,1)} %all-to-all-done.8.x_ref), custom_call_target="tpu_custom_call" | custom-call | flops 4000000000 | bytes 10000000 | tf_op jit(solution)/shard_map/place/pallas_call | solution.py:391
  767.1 17.7 %place.5.refs_0_ = bf16[16,73,8,1024]{3,2,1,0:T(8,128)(2,1)} custom-call(bf16[8,2,73,16,128]{4,3,2,1,0:T(8,128)(2,1)} %all-to-all-done.5.x_ref, bf16[16,73,8,1024]{3,2,1,0:T(8,128)(2,1)} %place.4.refs_0_), custom_call_target="tpu_custom_call", output_to_operand_aliasing={{}: (1, {})} | custom-call | flops 4000000000 | bytes 10000000 | tf_op jit(solution)/shard_map/place/pallas_call | solution.py:391
  784.8 17.7 %place.6.refs_0_ = bf16[16,73,8,1024]{3,2,1,0:T(8,128)(2,1)} custom-call(bf16[8,2,73,16,128]{4,3,2,1,0:T(8,128)(2,1)} %all-to-all-done.3.x_ref, bf16[16,73,8,1024]{3,2,1,0:T(8,128)(2,1)} %place.5.refs_0_), custom_call_target="tpu_custom_call", output_to_operand_aliasing={{}: (1, {})} | custom-call | flops 4000000000 | bytes 10000000 | tf_op jit(solution)/shard_map/place/pallas_call | solution.py:391
  804.7 17.7 %place.7 = bf16[16,73,8,1024]{3,2,1,0:T(8,128)(2,1)} custom-call(bf16[8,2,73,16,128]{4,3,2,1,0:T(8,128)(2,1)} %all-to-all-done.1.x_ref, bf16[16,73,8,1024]{3,2,1,0:T(8,128)(2,1)} %place.6.refs_0_), custom_call_target="tpu_custom_call", output_to_operand_aliasing={{}: (1, {})} | custom-call | flops 4000000000 | bytes 10000000 | tf_op jit(solution)/shard_map/place/pallas_call | solution.py:391
  (108 shorter events, 47.4 us)
Async XLA Ops:
  36.6 78.5 %all-to-all-start.6 = ((bf16[8,1,73,16,128]{4,3,2,1,0:T(8,128)(2,1)}), bf16[8,1,73,16,128]{4,3,2,1,0:T(8,128)(2,1)S(1)}, u32[]{:S(2)}, u32[]{:S(2)}) async-start(bf16[8,1,73,16,128]{4,3,2,1,0:T(8,128)(2,1)} %forecast.8), calls=%async_computation.6 | async-start | bytes 4784128 | tf_op jit(solution)/shard_map/all_to_all | solution.py:429
  48.3 19.5 %collective-permute-start.12 = (bf16[16,80,256]{2,1,0:T(8,128)(2,1)}, bf16[16,80,256]{2,1,0:T(8,128)(2,1)}, u32[]{:S(2)}, u32[]{:S(2)}) collective-permute-start(bf16[16,80,256]{2,1,0:T(8,128)(2,1)} %get-tuple-element.40), channel_id=1, source_target_pairs={{0,8},{8,16},{16,24},{24,0},{1,9},{9,17},{17,25},{25,1},{2,10},{10... | collective-permute-start | bytes 1966088 | tf_op jit(solution)/shard_map/ppermute | solution.py:406
  49.9 31.6 %collective-permute-start.13 = (bf16[16,80,256]{2,1,0:T(8,128)(2,1)}, bf16[16,80,256]{2,1,0:T(8,128)(2,1)}, u32[]{:S(2)}, u32[]{:S(2)}) collective-permute-start(bf16[16,80,256]{2,1,0:T(8,128)(2,1)} %get-tuple-element.41), channel_id=1, source_target_pairs={{0,24},{8,0},{16,8},{24,16},{1,25},{9,1},{17,9},{25,17},{2,26},{10... | collective-permute-start | bytes 1966088 | tf_op jit(solution)/shard_map/ppermute | solution.py:406
  58.6 60.9 %collective-permute-start.8 = (bf16[16,80,256]{2,1,0:T(8,128)(2,1)}, bf16[16,80,256]{2,1,0:T(8,128)(2,1)S(1)}, u32[]{:S(2)}, u32[]{:S(2)}) collective-permute-start(bf16[16,80,256]{2,1,0:T(8,128)(2,1)} %get-tuple-element.35), channel_id=1, source_target_pairs={{0,8},{8,16},{16,24},{24,0},{1,9},{9,17},{17,25},{25,1},{2,10},{10... | collective-permute-start | bytes 1966088 | tf_op jit(solution)/shard_map/ppermute | solution.py:406
  58.6 61.0 %collective-permute-start.9 = (bf16[16,80,256]{2,1,0:T(8,128)(2,1)}, bf16[16,80,256]{2,1,0:T(8,128)(2,1)}, u32[]{:S(2)}, u32[]{:S(2)}) collective-permute-start(bf16[16,80,256]{2,1,0:T(8,128)(2,1)} %get-tuple-element.36), channel_id=1, source_target_pairs={{0,24},{8,0},{16,8},{24,16},{1,25},{9,1},{17,9},{25,17},{2,26},{10... | collective-permute-start | bytes 1966088 | tf_op jit(solution)/shard_map/ppermute | solution.py:406
  115.1 61.0 %copy-start = (bf16[8,1,73,16,128]{4,3,2,1,0:T(8,128)(2,1)}, bf16[8,1,73,16,128]{4,3,2,1,0:T(8,128)(2,1)S(1)}, u32[]{:S(2)}) copy-start(bf16[8,1,73,16,128]{4,3,2,1,0:T(8,128)(2,1)S(1)} %all-to-all-done.6.refs_0_) | copy-start | bytes 7176196
  115.1 61.0 %all-to-all-start.7 = ((bf16[8,1,73,16,128]{4,3,2,1,0:T(8,128)(2,1)}), bf16[8,1,73,16,128]{4,3,2,1,0:T(8,128)(2,1)}, u32[]{:S(2)}, u32[]{:S(2)}) async-start(bf16[8,1,73,16,128]{4,3,2,1,0:T(8,128)(2,1)} %forecast.9), calls=%async_computation.7 | async-start | bytes 4784128 | tf_op jit(solution)/shard_map/all_to_all | solution.py:429
  119.5 0.8 copy-start.3
  176.1 99.0 %all-to-all-start.4 = ((bf16[8,2,73,16,128]{4,3,2,1,0:T(8,128)(2,1)}), bf16[8,2,73,16,128]{4,3,2,1,0:T(8,128)(2,1)}, u32[]{:S(2)}, u32[]{:S(2)}) async-start(bf16[8,2,73,16,128]{4,3,2,1,0:T(8,128)(2,1)} %forecast.7), calls=%async_computation.4 | async-start | bytes 9568256 | tf_op jit(solution)/shard_map/all_to_all | solution.py:429
  187.2 19.5 %collective-permute-start.4 = (bf16[16,80,256]{2,1,0:T(8,128)(2,1)}, bf16[16,80,256]{2,1,0:T(8,128)(2,1)S(1)}, u32[]{:S(2)}, u32[]{:S(2)}) collective-permute-start(bf16[16,80,256]{2,1,0:T(8,128)(2,1)} %get-tuple-element.30), channel_id=1, source_target_pairs={{0,8},{8,16},{16,24},{24,0},{1,9},{9,17},{17,25},{25,1},{2,10},{10... | collective-permute-start | bytes 1966088 | tf_op jit(solution)/shard_map/ppermute | solution.py:406
  188.0 30.5 %collective-permute-start.5 = (bf16[16,80,256]{2,1,0:T(8,128)(2,1)}, bf16[16,80,256]{2,1,0:T(8,128)(2,1)S(1)}, u32[]{:S(2)}, u32[]{:S(2)}) collective-permute-start(bf16[16,80,256]{2,1,0:T(8,128)(2,1)} %get-tuple-element.31), channel_id=1, source_target_pairs={{0,24},{8,0},{16,8},{24,16},{1,25},{9,1},{17,9},{25,17},{2,26},{10... | collective-permute-start | bytes 1966088 | tf_op jit(solution)/shard_map/ppermute | solution.py:406
  206.7 11.8 %copy-start.4 = (bf16[16,80,256]{2,1,0:T(8,128)(2,1)}, bf16[16,80,256]{2,1,0:T(8,128)(2,1)S(1)}, u32[]{:S(2)}) copy-start(bf16[16,80,256]{2,1,0:T(8,128)(2,1)S(1)} %collective-permute-done.4.refs_3_) | copy-start | bytes 1966084
  218.5 0.8 copy-start.5
  275.1 98.9 %all-to-all-start.2 = ((bf16[8,2,73,16,128]{4,3,2,1,0:T(8,128)(2,1)}), bf16[8,2,73,16,128]{4,3,2,1,0:T(8,128)(2,1)}, u32[]{:S(2)}, u32[]{:S(2)}) async-start(bf16[8,2,73,16,128]{4,3,2,1,0:T(8,128)(2,1)} %forecast.6), calls=%async_computation.2 | async-start | bytes 9568256 | tf_op jit(solution)/shard_map/all_to_all | solution.py:429
  279.7 10.4 %copy-start.6 = (f32[1024,8,16]{0,2,1:T(8,128)S(1)}, f32[1024,8,16]{0,2,1:T(8,128)}, u32[]{:S(2)}) copy-start(f32[1024,8,16]{0,2,1:T(8,128)} %param.11) | copy-start | bytes 1572868
  286.2 6.5 copy-start.7
  286.2 19.5 %collective-permute-start = (bf16[16,80,256]{2,1,0:T(8,128)(2,1)}, bf16[16,80,256]{2,1,0:T(8,128)(2,1)S(1)}, u32[]{:S(2)}, u32[]{:S(2)}) collective-permute-start(bf16[16,80,256]{2,1,0:T(8,128)(2,1)} %get-tuple-element.25), channel_id=1, source_target_pairs={{0,8},{8,16},{16,24},{24,0},{1,9},{9,17},{17,25},{25,1},{2,10},{10... | collective-permute-start | bytes 1966088 | tf_op jit(solution)/shard_map/ppermute | solution.py:406
  287.1 30.6 %collective-permute-start.1 = (bf16[16,80,256]{2,1,0:T(8,128)(2,1)}, bf16[16,80,256]{2,1,0:T(8,128)(2,1)S(1)}, u32[]{:S(2)}, u32[]{:S(2)}) collective-permute-start(bf16[16,80,256]{2,1,0:T(8,128)(2,1)} %get-tuple-element.26), channel_id=1, source_target_pairs={{0,24},{8,0},{16,8},{24,16},{1,25},{9,1},{17,9},{25,17},{2,26},{10... | collective-permute-start | bytes 1966088 | tf_op jit(solution)/shard_map/ppermute | solution.py:406
  305.7 12.0 %copy-start.1 = (bf16[16,80,256]{2,1,0:T(8,128)(2,1)}, bf16[16,80,256]{2,1,0:T(8,128)(2,1)S(1)}, u32[]{:S(2)}) copy-start(bf16[16,80,256]{2,1,0:T(8,128)(2,1)S(1)} %collective-permute-done.refs_3_) | copy-start | bytes 1966084
  317.8 0.9 copy-start.2
  374.0 96.2 %all-to-all-start = ((bf16[8,2,73,16,128]{4,3,2,1,0:T(8,128)(2,1)}), bf16[8,2,73,16,128]{4,3,2,1,0:T(8,128)(2,1)}, u32[]{:S(2)}, u32[]{:S(2)}) async-start(bf16[8,2,73,16,128]{4,3,2,1,0:T(8,128)(2,1)} %forecast.5), calls=%async_computation | async-start | bytes 9568256 | tf_op jit(solution)/shard_map/all_to_all | solution.py:429
  378.8 2.3 copy-start.8
  402.2 11.5 %collective-permute-start.14 = (f32[4,136,128]{2,1,0:T(8,128)}, f32[4,136,128]{2,1,0:T(8,128)S(1)}, u32[]{:S(2)}, u32[]{:S(2)}) collective-permute-start(f32[4,136,128]{2,1,0:T(8,128)} %get-tuple-element.43.gr_ref), channel_id=1, source_target_pairs={{0,8},{8,16},{16,24},{24,0},{1,9},{9,17},{17,25},{25,1},{2,10},{10... | collective-permute-start | bytes 835592 | tf_op jit(solution)/shard_map/ppermute | solution.py:406
  403.9 14.1 %collective-permute-start.15 = (f32[4,136,128]{2,1,0:T(8,128)}, f32[4,136,128]{2,1,0:T(8,128)S(1)}, u32[]{:S(2)}, u32[]{:S(2)}) collective-permute-start(f32[4,136,128]{2,1,0:T(8,128)} %get-tuple-element.42.gl_ref), channel_id=1, source_target_pairs={{0,24},{8,0},{16,8},{24,16},{1,25},{9,1},{17,9},{25,17},{2,26},{10... | collective-permute-start | bytes 835592 | tf_op jit(solution)/shard_map/ppermute | solution.py:406
  413.6 4.3 copy-start.9
  418.0 0.7 copy-start.13
  470.1 91.4 %all-to-all-start.8 = ((bf16[8,2,73,16,128]{4,3,2,1,0:T(8,128)(2,1)}), bf16[8,2,73,16,128]{4,3,2,1,0:T(8,128)(2,1)}, u32[]{:S(2)}, u32[]{:S(2)}) async-start(bf16[8,2,73,16,128]{4,3,2,1,0:T(8,128)(2,1)} %update.7), calls=%async_computation.8 | async-start | bytes 9568256 | tf_op jit(solution)/shard_map/all_to_all | solution.py:429
  493.9 11.4 %collective-permute-start.10 = (f32[4,136,128]{2,1,0:T(8,128)}, f32[4,136,128]{2,1,0:T(8,128)S(1)}, u32[]{:S(2)}, u32[]{:S(2)}) collective-permute-start(f32[4,136,128]{2,1,0:T(8,128)} %get-tuple-element.38.gr_ref), channel_id=1, source_target_pairs={{0,8},{8,16},{16,24},{24,0},{1,9},{9,17},{17,25},{25,1},{2,10},{10... | collective-permute-start | bytes 835592 | tf_op jit(solution)/shard_map/ppermute | solution.py:406
  495.1 14.4 %collective-permute-start.11 = (f32[4,136,128]{2,1,0:T(8,128)}, f32[4,136,128]{2,1,0:T(8,128)S(1)}, u32[]{:S(2)}, u32[]{:S(2)}) collective-permute-start(f32[4,136,128]{2,1,0:T(8,128)} %get-tuple-element.37.gl_ref), channel_id=1, source_target_pairs={{0,24},{8,0},{16,8},{24,16},{1,25},{9,1},{17,9},{25,17},{2,26},{10... | collective-permute-start | bytes 835592 | tf_op jit(solution)/shard_map/ppermute | solution.py:406
  505.4 4.1 copy-start.10
  509.4 0.7 copy-start.14
  561.6 91.6 %all-to-all-start.5 = ((bf16[8,2,73,16,128]{4,3,2,1,0:T(8,128)(2,1)}), bf16[8,2,73,16,128]{4,3,2,1,0:T(8,128)(2,1)}, u32[]{:S(2)}, u32[]{:S(2)}) async-start(bf16[8,2,73,16,128]{4,3,2,1,0:T(8,128)(2,1)} %update.6), calls=%async_computation.5 | async-start | bytes 9568256 | tf_op jit(solution)/shard_map/all_to_all | solution.py:429
  585.4 11.4 %collective-permute-start.6 = (f32[4,136,128]{2,1,0:T(8,128)}, f32[4,136,128]{2,1,0:T(8,128)S(1)}, u32[]{:S(2)}, u32[]{:S(2)}) collective-permute-start(f32[4,136,128]{2,1,0:T(8,128)} %get-tuple-element.33.gr_ref), channel_id=1, source_target_pairs={{0,8},{8,16},{16,24},{24,0},{1,9},{9,17},{17,25},{25,1},{2,10},{10... | collective-permute-start | bytes 835592 | tf_op jit(solution)/shard_map/ppermute | solution.py:406
  586.5 14.4 %collective-permute-start.7 = (f32[4,136,128]{2,1,0:T(8,128)}, f32[4,136,128]{2,1,0:T(8,128)S(1)}, u32[]{:S(2)}, u32[]{:S(2)}) collective-permute-start(f32[4,136,128]{2,1,0:T(8,128)} %get-tuple-element.32.gl_ref), channel_id=1, source_target_pairs={{0,24},{8,0},{16,8},{24,16},{1,25},{9,1},{17,9},{25,17},{2,26},{10... | collective-permute-start | bytes 835592 | tf_op jit(solution)/shard_map/ppermute | solution.py:406
  596.8 4.1 copy-start.11
  600.9 0.7 copy-start.15
  653.1 91.6 %all-to-all-start.3 = ((bf16[8,2,73,16,128]{4,3,2,1,0:T(8,128)(2,1)}), bf16[8,2,73,16,128]{4,3,2,1,0:T(8,128)(2,1)}, u32[]{:S(2)}, u32[]{:S(2)}) async-start(bf16[8,2,73,16,128]{4,3,2,1,0:T(8,128)(2,1)} %update.5), calls=%async_computation.3 | async-start | bytes 9568256 | tf_op jit(solution)/shard_map/all_to_all | solution.py:429
  676.9 11.4 %collective-permute-start.2 = (f32[4,136,128]{2,1,0:T(8,128)}, f32[4,136,128]{2,1,0:T(8,128)S(1)}, u32[]{:S(2)}, u32[]{:S(2)}) collective-permute-start(f32[4,136,128]{2,1,0:T(8,128)} %get-tuple-element.28.gr_ref), channel_id=1, source_target_pairs={{0,8},{8,16},{16,24},{24,0},{1,9},{9,17},{17,25},{25,1},{2,10},{10... | collective-permute-start | bytes 835592 | tf_op jit(solution)/shard_map/ppermute | solution.py:406
  678.1 14.4 %collective-permute-start.3 = (f32[4,136,128]{2,1,0:T(8,128)}, f32[4,136,128]{2,1,0:T(8,128)S(1)}, u32[]{:S(2)}, u32[]{:S(2)}) collective-permute-start(f32[4,136,128]{2,1,0:T(8,128)} %get-tuple-element.27.gl_ref), channel_id=1, source_target_pairs={{0,24},{8,0},{16,8},{24,16},{1,25},{9,1},{17,9},{25,17},{2,26},{10... | collective-permute-start | bytes 835592 | tf_op jit(solution)/shard_map/ppermute | solution.py:406
  688.4 4.1 copy-start.12
  692.5 0.7 copy-start.16
  744.7 59.9 %all-to-all-start.1 = ((bf16[8,2,73,16,128]{4,3,2,1,0:T(8,128)(2,1)}), bf16[8,2,73,16,128]{4,3,2,1,0:T(8,128)(2,1)}, u32[]{:S(2)}, u32[]{:S(2)}) async-start(bf16[8,2,73,16,128]{4,3,2,1,0:T(8,128)(2,1)} %update.4), calls=%async_computation.1 | async-start | bytes 9568256 | tf_op jit(solution)/shard_map/all_to_all | solution.py:429
